TPU v7x, 32 devices: a whole 2x2x4 slice. The times are simulated.
32 devices in a mesh: gx: 2 (over core), gy: 4 (over y, x), gz: 4 (over z).
Axes of the slice: x: 2, y: 2, z: 4, core: 2. Of those that a mesh axis runs over, the one named last changes fastest.
Arguments:
- block_values: bfloat16 [4, 64, 4, 6, 128, 128], P('gy', 'gx', 'gz'), as said below
- block_cols: int32 [4, 64, 4, 6], P('gy', 'gx', 'gz'), may hold values from 0 to 63, as said below
Outputs:
- purified: float32 [256, 32768], P(('gx', 'gy'), 'gz')
Inputs may be any that keep to these rules, and one draw needn't show every extreme that they name: block_cols[a, s, b, :] holds 6 distinct tile columns of panel b at which tile row a * 64 + s of P is nonzero; every tile column of a panel is listed by exactly 6 tile rows of each slab; the pattern is symmetric: tile (i, j) is listed exactly when tile (j, i) is. `block_values`: P is symmetric: the tile listed at (i, j) is the transpose of the tile listed at (j, i), and diagonal tiles are symmetric.
All inputs are finite; a program needn't handle non-finite values.
Results may differ from a plain program's by a relative error of at most 0.0033.
Values may be sent and summed in bfloat16 or wider, within the bound.
A program may use at most 128 MiB of HBM per device.

v0:
```python
import jax
import jax.numpy as jnp
from jax import lax
from jax.sharding import PartitionSpec as P

WIN = 1


def broadcast(value, axis, source):
    kept = jnp.where(lax.axis_index(axis) == source, value, 0).astype(value.dtype)
    return lax.psum(kept, axis)


def densify(left_tiles, left_columns, slab_tiles):
    onehot = (
        left_columns[:, :, None] == jnp.arange(slab_tiles, dtype=jnp.int32)[None, None, :]
    ).astype(jnp.bfloat16)
    densified = jnp.einsum("wkj,wkyx->wyjx", onehot, left_tiles, preferred_element_type=jnp.float32)
    tile_size = left_tiles.shape[2]
    return densified.astype(jnp.bfloat16).reshape(
        left_tiles.shape[0] * tile_size, slab_tiles, tile_size
    )


def product_one(left_panel, panel_tiles, panel_columns):
    summed = jnp.zeros(
        (left_panel.shape[0], panel_tiles.shape[0], panel_tiles.shape[2]), jnp.float32
    )
    for column_slot in range(panel_tiles.shape[1]):
        picked = jnp.take(left_panel, panel_columns[:, column_slot], axis=1)
        summed = summed + jnp.einsum(
            "rix,iyx->riy", picked, panel_tiles[:, column_slot], preferred_element_type=jnp.float32
        )
    return summed


def product_two(rounded, panel_tiles, panel_columns, panel_width):
    summed = jnp.zeros((rounded.shape[0], panel_width, panel_tiles.shape[3]), jnp.float32)
    for column_slot in range(panel_tiles.shape[1]):
        product = jnp.einsum(
            "rix,ixy->riy", rounded, panel_tiles[:, column_slot], preferred_element_type=jnp.float32
        )
        summed = summed.at[:, panel_columns[:, column_slot], :].add(product)
    return summed


def local(block_values, block_cols):
    tiles_here = block_values[0, :, 0]
    columns_here = block_cols[0, :, 0]
    tile_size = tiles_here.shape[2]
    slab_tiles = tiles_here.shape[0] * lax.axis_size("gx")
    left_tiles, left_columns = (
        broadcast(tiles_here[:WIN], "gy", 0),
        broadcast(columns_here[:WIN], "gy", 0),
    )
    left_panel = densify(left_tiles, left_columns, slab_tiles)
    height = left_panel.shape[0]
    on_diagonal = (lax.axis_index("gy") == lax.axis_index("gz")).astype(jnp.float32)
    panel_tiles, panel_columns = (
        lax.all_gather(tiles_here, "gx", axis=0, tiled=True),
        lax.all_gather(columns_here, "gx", axis=0, tiled=True),
    )
    partial_square = product_one(left_panel, panel_tiles, panel_columns)
    partial_square = partial_square.reshape(height, slab_tiles * tile_size)
    square = lax.psum(partial_square, "gz")
    square_low = square.astype(jnp.bfloat16).reshape(height, slab_tiles, tile_size)
    applied = product_two(square_low, panel_tiles, panel_columns, slab_tiles).reshape(
        lax.axis_size("gy") * (height // lax.axis_size("gy")), slab_tiles * tile_size
    )
    return lax.psum_scatter(
        3.0 * on_diagonal * square - 2.0 * applied, "gy", scatter_dimension=0, tiled=True
    )


def solution(mesh):
    in_specs = (P("gy", "gx", "gz", None, None, None), P("gy", "gx", "gz", None))
    out_specs = P(("gx", "gy"), "gz")
    return jax.shard_map(local, mesh=mesh, in_specs=in_specs, out_specs=out_specs, check_vma=False)
```

profile of v0, /device:TPU:0, one launch (start us, length us, event | category | flops | bytes accessed | tf_op | source)
XLA Modules:
  0.0 449.7 jit_solution(1277576746980991775)
XLA Ops:
  9.2 8.0 %copy.48 = bf16[1,32,1,6,128,128]{5,4,1,3,2,0:T(8,128)(2,1)} copy(bf16[1,32,1,6,128,128]{5,4,3,2,1,0:T(8,128)(2,1)} %param.4) | data formatting | bytes 12582912 | tf_op args[0]
  18.2 8.9 %psum.25 = s32[6]{0:T(128)S(1)} all-reduce(s32[6]{0:T(128)S(1)} %fusion.44), channel_id=1, replica_groups=mesh['gx'=2,'gy'=4,'gz'=4] {'gy'}, use_global_device_ids=true, to_apply=%region_1.2 | all-reduce | flops 6 | bytes 48 | tf_op jit(solution)/shard_map/psum | solution.py:11
  29.5 27.4 %all-reduce.3.cloned.1.call-done = bf16[6,128,128]{2,0,1:T(8,128)(2,1)} async-done(((bf16[6,128,128]{2,0,1:T(8,128)(2,1)}), bf16[6,128,128]{2,0,1:T(8,128)(2,1)}) %all-reduce.3.cloned.1.call-update) | async-done | bytes 196624 | tf_op jit(solution)/shard_map/psum | solution.py:11
  60.0 2.2 gather_fusion.4
  64.4 2.2 gather_fusion.2
  68.7 2.2 gather_fusion
  73.0 6.2 %fusion.1 = f32[64,128,128]{1,2,0:T(8,128)} fusion(bf16[64,128,128]{2,1,0:T(8,128)(2,1)} %gather_fusion.4, pred[64]{0:T(512)(128)(4,1)S(1)} %get-tuple-element.24, bf16[64,6,128,128]{3,2,0,1:T(8,128)(2,1)} %bitcast.77), kind=kOutput, calls=%fused_computation.21 | convolution fusion | flops 269484032 | bytes 8388672 | tf_op jit(solution)/shard_map/rix,iyx->riy/dot_general | solution.py:31
  79.1 6.0 %fusion.3 = f32[64,128,128]{1,2,0:T(8,128)} fusion(bf16[64,128,128]{2,1,0:T(8,128)(2,1)} %gather_fusion.3, pred[64]{0:T(512)(128)(4,1)S(1)} %get-tuple-element.25, bf16[64,6,128,128]{3,2,0,1:T(8,128)(2,1)} %bitcast.78), kind=kOutput, calls=%fused_computation.23 | convolution fusion | flops 269484032 | bytes 8388672 | tf_op jit(solution)/shard_map/rix,iyx->riy/dot_general | solution.py:31
  85.2 3.6 fusion.5
  88.8 3.6 fusion.7
  92.4 3.6 fusion.9
  96.0 10.1 %add_add_fusion = f32[64,128,128]{1,2,0:T(8,128)} fusion(f32[64,128,128]{1,2,0:T(8,128)} %fusion.1, f32[64,128,128]{1,2,0:T(8,128)} %fusion.3, f32[64,128,128]{1,2,0:T(8,128)} %fusion.5, f32[64,128,128]{1,2,0:T(8,128)} %fusion.9, f32[64,128,128]{1,2,0:T(8,128)} %fusion.7, bf16[64,128,128]{2,1,0:T(8,128)(2,1)S(1)} %copy-done.4, ...), kind=kOutput, calls=%fused_computation.13 | convolution fusion | flops 274726912 | bytes 29360640 | tf_op jit(solution)/shard_map/rix,iyx->riy/dot_general | solution.py:31
  106.4 154.9 %all-reduce.5.cloned.1.call-done = f32[128,8192]{0,1:T(8,128)} async-done(((f32[128,8192]{0,1:T(8,128)}), f32[128,8192]{0,1:T(8,128)}) %all-reduce.5.cloned.1.call-update) | async-done | bytes 4194320 | tf_op jit(solution)/shard_map/psum | solution.py:65
  261.3 2.5 convert_element_type.19
  263.8 4.5 %fusion.24 = f32[64,128,128]{2,1,0:T(8,128)} fusion(bf16[128,64,128]{0,2,1:T(8,128)(2,1)S(1)} %bitcast.71, bf16[64,6,128,128]{3,2,0,1:T(8,128)(2,1)} %bitcast.79), kind=kOutput, calls=%fused_computation.46 | convolution fusion | flops 268435456 | bytes 8388608 | tf_op jit(solution)/shard_map/rix,ixy->riy/dot_general | solution.py:40
  268.4 4.6 %fusion.23 = f32[64,128,128]{2,1,0:T(8,128)} fusion(bf16[128,64,128]{0,2,1:T(8,128)(2,1)S(1)} %bitcast.72, bf16[64,6,128,128]{3,2,0,1:T(8,128)(2,1)} %bitcast.80), kind=kOutput, calls=%fused_computation.45 | convolution fusion | flops 268435456 | bytes 8388608 | tf_op jit(solution)/shard_map/rix,ixy->riy/dot_general | solution.py:40
  272.9 2.8 fusion.25
  275.8 2.8 fusion.26
  278.6 2.8 fusion.27
  281.4 2.8 fusion.28
  284.2 2.5 broadcast_in_dim.30
  286.7 13.9 %scatter_fusion = f32[128,64,128]{2,0,1:T(8,128)} fusion(f32[128,64,128]{2,0,1:T(8,128)} %broadcast_in_dim.30, s32[64]{0:T(128)S(1)} %get-tuple-element.7, f32[64,128,128]{2,1,0:T(8,128)} %fusion.23), kind=kCustom, calls=%fused_computation.6 | custom fusion | flops 1048576 | bytes 12583168 | tf_op jit(solution)/shard_map/scatter-add | solution.py:43
  300.6 13.6 %scatter_fusion.1 = f32[128,64,128]{2,0,1:T(8,128)} fusion(f32[128,64,128]{2,0,1:T(8,128)} %scatter_fusion, s32[64]{0:T(128)S(1)} %get-tuple-element.8, f32[64,128,128]{2,1,0:T(8,128)} %fusion.24), kind=kCustom, calls=%fused_computation.7 | custom fusion | flops 1048576 | bytes 12583168 | tf_op jit(solution)/shard_map/scatter-add | solution.py:43
  314.2 13.6 %scatter_fusion.2 = f32[128,64,128]{2,0,1:T(8,128)} fusion(f32[128,64,128]{2,0,1:T(8,128)} %scatter_fusion.1, s32[64]{0:T(128)S(1)} %get-tuple-element.9, f32[64,128,128]{2,1,0:T(8,128)} %fusion.25), kind=kCustom, calls=%fused_computation.8 | custom fusion | flops 1048576 | bytes 12583168 | tf_op jit(solution)/shard_map/scatter-add | solution.py:43
  327.8 13.6 %scatter_fusion.3 = f32[128,64,128]{2,0,1:T(8,128)} fusion(f32[128,64,128]{2,0,1:T(8,128)} %scatter_fusion.2, s32[64]{0:T(128)S(1)} %get-tuple-element.10, f32[64,128,128]{2,1,0:T(8,128)} %fusion.26), kind=kCustom, calls=%fused_computation.9 | custom fusion | flops 1048576 | bytes 12583168 | tf_op jit(solution)/shard_map/scatter-add | solution.py:43
  341.4 13.7 %scatter_fusion.4 = f32[128,64,128]{2,0,1:T(8,128)} fusion(f32[128,64,128]{2,0,1:T(8,128)} %scatter_fusion.3, s32[64]{0:T(128)S(1)} %get-tuple-element.11, f32[64,128,128]{2,1,0:T(8,128)} %fusion.27), kind=kCustom, calls=%fused_computation.10 | custom fusion | flops 1048576 | bytes 12583168 | tf_op jit(solution)/shard_map/scatter-add | solution.py:43
  355.1 13.7 %scatter_fusion.5 = f32[128,64,128]{2,0,1:T(8,128)} fusion(f32[128,64,128]{2,0,1:T(8,128)} %scatter_fusion.4, s32[64]{0:T(128)S(1)} %get-tuple-element.6, f32[64,128,128]{2,1,0:T(8,128)} %fusion.28), kind=kCustom, calls=%fused_computation.11 | custom fusion | flops 1048576 | bytes 12583168 | tf_op jit(solution)/shard_map/scatter-add | solution.py:43
  368.8 4.7 %broadcast_multiply_fusion = f32[128,64,128]{2,0,1:T(8,128)} fusion(f32[128,64,128]{2,0,1:T(8,128)} %scatter_fusion.5), kind=kLoop, calls=%fused_computation.37 | loop fusion | flops 1048576 | bytes 8388608 | tf_op jit(solution)/shard_map/mul | solution.py:71
  373.6 5.6 %copy.60 = f32[128,64,128]{0,2,1:T(8,128)} copy(f32[128,64,128]{2,0,1:T(8,128)} %broadcast_multiply_fusion) | data formatting | bytes 8388608 | tf_op jit(solution)/shard_map/mul | solution.py:71
  379.2 5.8 %bitcast_subtract_fusion = f32[128,8192]{0,1:T(8,128)} fusion(f32[128,64,128]{0,2,1:T(8,128)} %copy.60, f32[128,8192]{0,1:T(8,128)} %all-reduce.5.cloned.1.call-done, f32[]{:T(128)S(6)} %mul_shard_map.3), kind=kLoop, calls=%fused_computation.12 | loop fusion | flops 2097152 | bytes 12582916 | tf_op jit(solution)/shard_map/sub | solution.py:71
  385.0 5.6 %copy.68 = f32[128,8192]{1,0:T(8,128)} copy(f32[128,8192]{0,1:T(8,128)} %bitcast_subtract_fusion) | data formatting | bytes 8388608
  390.7 51.9 %reduce-scatter.4.cloned.1.call-done = f32[32,8192]{1,0:T(8,128)} async-done(((f32[128,8192]{1,0:T(8,128)}), f32[32,8192]{1,0:T(8,128)}) %reduce-scatter.4.cloned.1.call-update) | async-done | bytes 1048592 | tf_op jit(solution)/shard_map/reduce_scatter | solution.py:70
  (52 shorter events, 14.9 us)
Async XLA Ops:
  7.4 49.5 %all-reduce.3.cloned.1.call-start = ((), (), s32[]{:S(2)}) async-start(), calls=%async_computation.1 | async-start | bytes 524288 | tf_op jit(solution)/shard_map/psum | solution.py:11
  9.2 63.8 %all-gather.4.cloned.1.call-start = ((), (), s32[]{:S(2)}) async-start(), calls=%async_computation.3 | async-start | bytes 18874368 | tf_op jit(solution)/shard_map/all_gather | solution.py:60
  17.3 0.7 copy-start.5
  17.3 244.0 %all-reduce.5.cloned.1.call-start = ((), (), s32[]{:S(2)}) async-start(), calls=%async_computation.2 | async-start | bytes 8388608 | tf_op jit(solution)/shard_map/psum | solution.py:65
  73.0 12.2 %copy-start = (bf16[1,64,1,6,128,128]{5,4,1,3,2,0:T(8,128)(2,1)S(1)}, bf16[1,64,1,6,128,128]{5,4,1,3,2,0:T(8,128)(2,1)}, u32[]{:S(2)}) copy-start(bf16[1,64,1,6,128,128]{5,4,1,3,2,0:T(8,128)(2,1)} %all-gather.4.cloned.1.call-done) | copy-start | bytes 37748740
  79.1 6.0 %copy-start.3 = (bf16[64,128,128]{2,1,0:T(8,128)(2,1)S(1)}, bf16[64,128,128]{2,1,0:T(8,128)(2,1)}, u32[]{:S(2)}) copy-start(bf16[64,128,128]{2,1,0:T(8,128)(2,1)} %gather_fusion.2) | copy-start | bytes 6291460
  85.2 3.6 copy-start.2
  88.8 3.6 copy-start.1
  92.4 3.6 copy-start.4
  106.1 336.4 %reduce-scatter.4.cloned.1.call-start = ((), (), s32[]{:S(2)}) async-start(), calls=%async_computation.4 | async-start | bytes 5242880 | tf_op jit(solution)/shard_map/reduce_scatter | solution.py:70
  261.3 11.7 %slice-start = ((s8[12582912]{0:T(1024)(128)(4,1)}), s8[4194304]{0:T(1024)(128)(4,1)S(1)}, s32[]{:S(2)}) async-start(s8[12582912]{0:T(1024)(128)(4,1)} %bitcast.85), calls=%async_computation.5 | async-start | bytes 8388608
  263.8 9.1 %slice-start.1 = ((s8[12582912]{0:T(1024)(128)(4,1)}), s8[4194304]{0:T(1024)(128)(4,1)S(1)}, s32[]{:S(2)}) async-start(s8[12582912]{0:T(1024)(128)(4,1)} %bitcast.85), calls=%async_computation.6 | async-start | bytes 8388608
  268.3 4.6 %slice-start.2 = ((s8[12582912]{0:T(1024)(128)(4,1)}), s8[4194304]{0:T(1024)(128)(4,1)S(1)}, s32[]{:S(2)}) async-start(s8[12582912]{0:T(1024)(128)(4,1)} %bitcast.85), calls=%async_computation.7 | async-start | bytes 8388608
Sparse Core Ops, SparseCore 0:
  11.1 45.7 all-reduce.2
  106.3 154.9 all-reduce.4
  390.8 51.6 reduce-scatter.3
Sparse Core Ops, SparseCore 1:
  17.4 27.3 all-gather.3
where the time goes:
time: 451 us; the launch traced here: 450 us
  waiting for transfers between devices  234 us (52%)
  other arithmetic  96.8 us (21%)
  matrix products  55.3 us (12%)
  local copies, waits for them, and re-layouts  37.7 us (8%)
  between operations  14.7 us (3%)
  blocking collectives  10.7 us (2%)
    psum x1, waiting for transfers between devices, local(): square = lax.psum(partial_square, 'gz')  155 us
    scatter-add x6, other arithmetic, product_two(): summed = summed.at[:, panel_columns[:, column_slot], :].add(product)  82.1 us
    reduce_scatter x1, waiting for transfers between devices, local(): lax.psum_scatter(3.0 * on_diagonal * square - 2.0 * applied, 'gy', scatte...  51.9 us
    dot_general x6, matrix products, product_one(): jnp.einsum('rix,iyx->riy', picked, panel_tiles[:, column_slot], preferred...  33.1 us
    psum x1, waiting for transfers between devices, broadcast(): return lax.psum(kept, axis)  27.4 us
    dot_general x6, matrix products, product_two(): jnp.einsum('rix,ixy->riy', rounded, panel_tiles[:, column_slot], preferre...  20.4 us
    unnamed x21, local copies, waits for them, and re-layouts  14.4 us
    gather x6, local copies, waits for them, and re-layouts, product_one(): picked = jnp.take(left_panel, panel_columns[:, column_slot], axis=1)  12.9 us
  transfers between devices with their start and end apart: 4, of which 3 were waited for; matrix products, arithmetic and copies ran while one was open for 6% of the time, Pallas kernels for 0%

commit v1 on v0

v1 whole, which is shorter than its diff:
```python
import functools

import jax
import jax.numpy as jnp
from jax import lax
from jax.experimental import pallas as pl
from jax.experimental.pallas import tpu as pltpu
from jax.sharding import PartitionSpec as P

WIN = 1
LANES = 128
MESH = pl.DeviceIdType.MESH


def pieces_of(count, most):
    for pieces in range(min(count, most), 0, -1):
        if count % pieces == 0:
            return pieces


def greet(axes):
    barrier = pltpu.get_barrier_semaphore()
    total = 0
    for axis in axes:
        size = lax.axis_size(axis)
        me = lax.axis_index(axis)
        for step in range(1, size):
            pl.semaphore_signal(
                barrier, inc=1, device_id={axis: lax.rem(me + step, size)}, device_id_type=MESH
            )
        total += size - 1
    pl.semaphore_wait(barrier, total)


def remote(src, dst, send, recv, axis, peer):
    return pltpu.make_async_remote_copy(
        src_ref=src, dst_ref=dst, send_sem=send, recv_sem=recv,
        device_id={axis: peer}, device_id_type=MESH,
    )


def gather_kernel(
    n_gx, n_gy, pieces, tiles, cols, panel, panel_cols, left, left_cols,
    stage, load_sem, own_sem, send_sem, recv_sem, col_own, col_send, col_recv,
    win_own, win_send, win_recv,
):
    gx, gy = lax.axis_index("gx"), lax.axis_index("gy")
    rows = tiles.shape[0]
    part = rows // pieces
    loads = []
    for p in range(pieces):
        span = pl.ds(p * part, part)
        loads.append(pltpu.make_async_copy(tiles.at[span], stage.at[span], load_sem.at[p]))
        loads[-1].start()
    greet(("gx", "gy"))
    window = stage.at[pl.ds(0, WIN)]
    col_copies = [pltpu.make_async_copy(cols, panel_cols.at[gx], col_own)]
    for step in range(1, n_gx):
        col_copies.append(
            remote(cols, panel_cols.at[gx], col_send.at[step], col_recv.at[step],
                   "gx", lax.rem(gx + step, n_gx))
        )
    for copy in col_copies:
        copy.start()
    copies = []
    for p in range(pieces):
        loads[p].wait()
        if p == 0:
            @pl.when(gy == 0)
            def _():
                for peer in range(1, n_gy):
                    remote(window, left, win_send.at[0, peer], win_recv.at[0], "gy", peer).start()
                    remote(cols, left_cols, win_send.at[1, peer], win_recv.at[1], "gy", peer).start()
                pltpu.make_async_copy(window, left, win_own.at[0]).start()
                pltpu.make_async_copy(cols, left_cols, win_own.at[1]).start()
        source = stage.at[pl.ds(p * part, part)]
        target = panel.at[pl.ds(gx * rows + p * part, part)]
        for step in range(1, n_gx):
            copy = remote(source, target, send_sem.at[step, p], recv_sem.at[step, p],
                          "gx", lax.rem(gx + step, n_gx))
            copy.start()
            copies.append(copy)
        copy = pltpu.make_async_copy(source, target, own_sem.at[p])
        copy.start()
        copies.append(copy)
    for copy in col_copies + copies:
        copy.wait()

    @pl.when(gy == 0)
    def _():
        for peer in range(1, n_gy):
            remote(window, left, win_send.at[0, peer], win_recv.at[0], "gy", peer).wait_send()
            remote(cols, left_cols, win_send.at[1, peer], win_recv.at[1], "gy", peer).wait_send()
        pltpu.make_async_copy(window, left, win_own.at[0]).wait()
        pltpu.make_async_copy(cols, left_cols, win_own.at[1]).wait()

    @pl.when(gy != 0)
    def _():
        remote(window, left, win_send.at[0, 0], win_recv.at[0], "gy", 0).wait_recv()
        remote(cols, left_cols, win_send.at[1, 0], win_recv.at[1], "gy", 0).wait_recv()


def gather(tiles, cols):
    n_gx, n_gy = lax.axis_size("gx"), lax.axis_size("gy")
    rows = tiles.shape[0]
    pieces = pieces_of(rows, 4)
    padded = jnp.pad(cols, ((0, 0), (0, LANES - cols.shape[1])))
    dma = pltpu.SemaphoreType.DMA
    return pl.pallas_call(
        functools.partial(gather_kernel, n_gx, n_gy, pieces),
        out_shape=(
            jax.ShapeDtypeStruct((n_gx * rows,) + tiles.shape[1:], tiles.dtype),
            jax.ShapeDtypeStruct((n_gx,) + padded.shape, padded.dtype),
            jax.ShapeDtypeStruct((WIN,) + tiles.shape[1:], tiles.dtype),
            jax.ShapeDtypeStruct(padded.shape, padded.dtype),
        ),
        in_specs=[
            pl.BlockSpec(memory_space=pl.ANY),
            pl.BlockSpec(memory_space=pltpu.VMEM),
        ],
        out_specs=[pl.BlockSpec(memory_space=pl.ANY)] * 4,
        scratch_shapes=[
            pltpu.VMEM(tiles.shape, tiles.dtype),
            dma((pieces,)), dma((pieces,)), dma((n_gx, pieces)), dma((n_gx, pieces)),
            dma, dma((n_gx,)), dma((n_gx,)),
            dma((2,)), dma((2, n_gy)), dma((2,)),
        ],
        compiler_params=pltpu.CompilerParams(collective_id=0, has_side_effects=True),
        name="gather_tiles",
    )(tiles, padded)


def first_kernel(block, slots, left_cols, panel_cols, left, tiles, out, dense):
    step = pl.program_id(0)

    @pl.when(step == 0)
    def _():
        dense[...] = jnp.zeros_like(dense)
        for k in range(slots):
            dense[left_cols[k]] = left[k]

    for r in range(block):
        base = (step * block + r) * slots
        picked = jnp.concatenate([dense[panel_cols[base + k]] for k in range(slots)], axis=1)
        held = jnp.concatenate([tiles[r, k] for k in range(slots)], axis=1)
        product = lax.dot_general(
            picked, held, (((1,), (1,)), ((), ())), preferred_element_type=jnp.float32
        )
        out[r] = product.astype(out.dtype)


def first(left, left_cols, panel, panel_cols):
    count, slots, size = panel.shape[0], panel.shape[1], panel.shape[2]
    block = pieces_of(count, 8)
    return pl.pallas_call(
        functools.partial(first_kernel, block, slots),
        out_shape=jax.ShapeDtypeStruct((count, size, size), panel.dtype),
        grid=(count // block,),
        in_specs=[
            pl.BlockSpec(memory_space=pltpu.SMEM),
            pl.BlockSpec(memory_space=pltpu.SMEM),
            pl.BlockSpec(left.shape, lambda i: (0, 0, 0)),
            pl.BlockSpec((block, slots, size, size), lambda i: (i, 0, 0, 0)),
        ],
        out_specs=pl.BlockSpec((block, size, size), lambda i: (i, 0, 0)),
        scratch_shapes=[pltpu.VMEM((count, size, size), panel.dtype)],
        compiler_params=pltpu.CompilerParams(dimension_semantics=("arbitrary",)),
        name="square_partial",
    )(left_cols, panel_cols, left, panel)


def reduce_kernel(size, pieces, part, own, out, landed, send_a, recv_a, send_b, recv_b):
    me = lax.axis_index("gz")
    step_rows = part.shape[0] // size
    rows = step_rows // pieces
    greet(("gz",))
    scatters, gathers = [], []
    for p in range(pieces):
        for d in range(1, size):
            peer = lax.rem(me + d, size)
            copy = remote(
                part.at[pl.ds(peer * step_rows + p * rows, rows)], landed.at[d - 1, p],
                send_a.at[d - 1, p], recv_a.at[d - 1, p], "gz", peer,
            )
            copy.start()
            scatters.append(copy)
    for p in range(pieces):
        for d in range(1, size):
            scatters[p * (size - 1) + d - 1].wait_recv()
        start = me * step_rows + p * rows
        for r in range(rows):
            total = part[start + r].astype(jnp.float32)
            for d in range(1, size):
                total = total + landed[d - 1, p, r].astype(jnp.float32)
            out[start + r] = total.astype(out.dtype)
        span = pl.ds(start, rows)
        for d in range(1, size):
            copy = remote(
                out.at[span], out.at[span],
                send_b.at[d - 1, p], recv_b.at[d - 1, p], "gz", lax.rem(me + d, size),
            )
            copy.start()
            gathers.append(copy)
    for copy in scatters:
        copy.wait_send()
    for copy in gathers:
        copy.wait()


def reduce_square(part):
    size = lax.axis_size("gz")
    step_rows = part.shape[0] // size
    pieces = pieces_of(step_rows, 4)
    dma = pltpu.SemaphoreType.DMA
    landed = (size - 1, pieces, step_rows // pieces) + part.shape[1:]

    def body(part_ref, out, landed_ref, *sems):
        reduce_kernel(size, pieces, part_ref, None, out, landed_ref, *sems)

    return pl.pallas_call(
        body,
        out_shape=jax.ShapeDtypeStruct(part.shape, part.dtype),
        in_specs=[pl.BlockSpec(memory_space=pltpu.VMEM)],
        out_specs=pl.BlockSpec(memory_space=pltpu.VMEM),
        scratch_shapes=[pltpu.VMEM(landed, part.dtype)] + [dma((size - 1, pieces))] * 4,
        compiler_params=pltpu.CompilerParams(collective_id=1, has_side_effects=True),
        name="square_reduce",
    )(part)


def second_kernel(block, slots, groups, panel_cols, square, tiles, out, total):
    step = pl.program_id(0)
    count = total.shape[0]
    height = total.shape[1] // groups

    @pl.when(step == 0)
    def _():
        total[...] = jnp.zeros_like(total)

    for r in range(block):
        row = step * block + r
        base = row * slots
        for k in range(0, slots, 2):
            held = jnp.concatenate([tiles[r, j] for j in range(k, min(k + 2, slots))], axis=1)
            product = jnp.dot(square[row], held, preferred_element_type=jnp.float32)
            for j in range(k, min(k + 2, slots)):
                width = tiles.shape[3]
                total[panel_cols[base + j]] += product[:, (j - k) * width:(j - k + 1) * width]

    @pl.when(step == pl.num_programs(0) - 1)
    def _():
        same = (lax.axis_index("gy") == lax.axis_index("gz")).astype(jnp.float32)

        @pl.loop(0, count)
        def _(c):
            value = (3.0 * same) * square[c].astype(jnp.float32) - 2.0 * total[c]
            value = value.astype(out.dtype)
            for g in range(groups):
                out[g, c] = value[g * height:(g + 1) * height]


def second(square, panel, panel_cols):
    count, slots, size = panel.shape[0], panel.shape[1], panel.shape[2]
    groups = lax.axis_size("gy")
    block = pieces_of(count, 8)
    shape = (groups, count, size // groups, size)
    return pl.pallas_call(
        functools.partial(second_kernel, block, slots, groups),
        out_shape=jax.ShapeDtypeStruct(shape, panel.dtype),
        grid=(count // block,),
        in_specs=[
            pl.BlockSpec(memory_space=pltpu.SMEM),
            pl.BlockSpec(square.shape, lambda i: (0, 0, 0)),
            pl.BlockSpec((block, slots, size, size), lambda i: (i, 0, 0, 0)),
        ],
        out_specs=pl.BlockSpec(shape, lambda i: (0, 0, 0, 0)),
        scratch_shapes=[pltpu.VMEM((count, size, size), jnp.float32)],
        compiler_params=pltpu.CompilerParams(dimension_semantics=("arbitrary",)),
        name="cube_partial",
    )(panel_cols, square, panel)


def scatter_kernel(size, pieces, part, out, landed, send, recv):
    me = lax.axis_index("gy")
    rows = part.shape[1] // pieces
    width = part.shape[3]
    greet(("gy",))
    copies = []
    for p in range(pieces):
        span = pl.ds(p * rows, rows)
        for d in range(1, size):
            peer = lax.rem(me + d, size)
            copy = remote(part.at[peer, span], landed.at[d - 1, p],
                          send.at[d - 1, p], recv.at[d - 1, p], "gy", peer)
            copy.start()
            copies.append(copy)
    for p in range(pieces):
        for d in range(1, size):
            copies[p * (size - 1) + d - 1].wait_recv()
        for r in range(rows):
            c = p * rows + r
            total = part[me, c].astype(jnp.float32)
            for d in range(1, size):
                total = total + landed[d - 1, p, r].astype(jnp.float32)
            out[:, c * width:(c + 1) * width] = total
    for copy in copies:
        copy.wait_send()


def scatter_result(part):
    size = lax.axis_size("gy")
    count, height, width = part.shape[1:]
    pieces = pieces_of(count, 4)
    dma = pltpu.SemaphoreType.DMA
    return pl.pallas_call(
        functools.partial(scatter_kernel, size, pieces),
        out_shape=jax.ShapeDtypeStruct((height, count * width), jnp.float32),
        in_specs=[pl.BlockSpec(memory_space=pltpu.VMEM)],
        out_specs=pl.BlockSpec(memory_space=pltpu.VMEM),
        scratch_shapes=[
            pltpu.VMEM((size - 1, pieces, count // pieces, height, width), part.dtype),
            dma((size - 1, pieces)), dma((size - 1, pieces)),
        ],
        compiler_params=pltpu.CompilerParams(collective_id=2, has_side_effects=True),
        name="result_scatter",
    )(part)


def local(block_values, block_cols):
    tiles = block_values[0, :, 0]
    cols = block_cols[0, :, 0]
    slots = cols.shape[1]
    panel, panel_cols, left, left_cols = gather(tiles, cols)
    panel_cols = panel_cols[:, :, :slots].reshape(-1)
    left_cols = left_cols[0, :slots]
    part = first(left[0], left_cols, panel, panel_cols)
    square = reduce_square(part)
    return scatter_result(second(square, panel, panel_cols))


def solution(mesh):
    in_specs = (P("gy", "gx", "gz", None, None, None), P("gy", "gx", "gz", None))
    out_specs = P(("gx", "gy"), "gz")
    return jax.shard_map(local, mesh=mesh, in_specs=in_specs, out_specs=out_specs, check_vma=False)
```

time: 451 us -> 169 us (0.37)
  waiting for transfers between devices: 234 us -> 0 us
  Pallas kernels: 0 us -> 161 us
  other arithmetic: 96.8 us -> 0 us
  matrix products: 55.3 us -> 0 us
  local copies, waits for them, and re-layouts: 37.7 us -> 6.37 us
  between operations: 14.7 us -> 0.03 us
  blocking collectives: 10.7 us -> 0 us
    psum x2 -> x0, waiting for transfers between devices: 182 us -> none  [the longest x1 155 us: local(): square = lax.psum(partial_square, 'gz')]
    pallas_call x0 -> x5, Pallas kernels: none -> 161 us  [the longest x1 95.6 us: reduce_square(): pl.pallas_call(body, out_shape=jax.ShapeDtypeStruct(part.shape, part.dtyp...]
    scatter-add x6 -> x0, other arithmetic: 82.1 us -> none  [product_two(): summed = summed.at[:, panel_columns[:, column_slot], :].add(product)]
    dot_general x13 -> x0, matrix products: 55.3 us -> none  [the longest x6 33.1 us: product_one(): jnp.einsum('rix,iyx->riy', picked, panel_tiles[:, column_slot], preferred...]
    reduce_scatter x1 -> x0, waiting for transfers between devices: 51.9 us -> none  [local(): lax.psum_scatter(3.0 * on_diagonal * square - 2.0 * applied, 'gy', scatte...]
    gather x6 -> x0, local copies, waits for them, and re-layouts: 12.9 us -> none  [product_one(): picked = jnp.take(left_panel, panel_columns[:, column_slot], axis=1)]
    unnamed x21 -> x2, local copies, waits for them, and re-layouts: 14.4 us -> 3.03 us
    psum x1 -> x0, blocking collectives: 8.89 us -> none  [broadcast(): return lax.psum(kept, axis)]
  transfers between devices with their start and end apart: 4 -> 0, of which waited for: 3 -> 0; matrix products, arithmetic and copies ran while one was open for 6% -> 0% of each run, Pallas kernels for 0% -> 0%
where the time goes in v1:
time: 169 us; the launch traced here: 168 us
  Pallas kernels  161 us (95%)
  local copies, waits for them, and re-layouts  6.37 us (4%)
    pallas_call x1, Pallas kernels, reduce_square(): pl.pallas_call(body, out_shape=jax.ShapeDtypeStruct(part.shape, part.dtyp...  95.6 us
    pallas_call x1, Pallas kernels, scatter_result(): pl.pallas_call(functools.partial(scatter_kernel, size, pieces), out_shape...  28 us
    pallas_call x1, Pallas kernels, gather(): pl.pallas_call(functools.partial(gather_kernel, n_gx, n_gy, pieces), out_...  15 us
    pallas_call x1, Pallas kernels, second(): pl.pallas_call(functools.partial(second_kernel, block, slots, groups), ou...  12.3 us
    pallas_call x1, Pallas kernels, first(): pl.pallas_call(functools.partial(first_kernel, block, slots), out_shape=j...  10.2 us

profile of v1, /device:TPU:0, one launch (start us, length us, event | category | flops | bytes accessed | tf_op | source)
XLA Modules:
  0.0 167.5 jit_solution(10354972001375685432)
XLA Ops:
  0.0 0.8 copy.4
  0.8 0.6 pad.4.cols
  1.4 15.0 %gather_tiles.1 = (bf16[64,6,128,128]{3,2,1,0:T(8,128)(2,1)}, s32[2,32,128]{2,1,0:T(8,128)}, bf16[1,6,128,128]{3,2,1,0:T(8,128)(2,1)}, s32[32,128]{1,0:T(8,128)}) custom-call(bf16[32,6,128,128]{3,2,1,0:T(8,128)(2,1)} %bitcast.6, s32[32,128]{1,0:T(8,128)} %pad.4.cols), custom_call_target="tpu_custom_call" | custom-call | tf_op jit(solution)/shard_map/gather_tiles/pallas_call | solution.py:109
  16.3 1.5 reshape.3.panel_cols
  17.8 1.3 slice_bitcast_fusion.left_cols
  19.1 10.2 %square_partial.1.part_ref = bf16[64,128,128]{2,1,0:T(8,128)(2,1)} custom-call(s32[6]{0:T(128)} %slice_bitcast_fusion.left_cols, s32[384]{0:T(512)} %reshape.3.panel_cols, bf16[6,128,128]{2,1,0:T(8,128)(2,1)} %bitcast.7, bf16[64,6,128,128]{3,2,1,0:T(8,128)(2,1)} %get-tuple-element.12.tiles), custom_call_target="tpu_custom_call" | custom-call | tf_op jit(solution)/shard_map/square_partial/pallas_call | solution.py:155
  29.3 95.6 %square_reduce.1.square = bf16[64,128,128]{2,1,0:T(8,128)(2,1)} custom-call(bf16[64,128,128]{2,1,0:T(8,128)(2,1)} %square_partial.1.part_ref), custom_call_target="tpu_custom_call" | custom-call | tf_op jit(solution)/shard_map/square_reduce/pallas_call | solution.py:220
  124.9 12.3 %cube_partial.1.part = bf16[4,64,32,128]{3,2,1,0:T(8,128)(2,1)} custom-call(s32[384]{0:T(512)} %reshape.3.panel_cols, bf16[64,128,128]{2,1,0:T(8,128)(2,1)} %square_reduce.1.square, bf16[64,6,128,128]{3,2,1,0:T(8,128)(2,1)} %get-tuple-element.12.tiles), custom_call_target="tpu_custom_call" | custom-call | tf_op jit(solution)/shard_map/cube_partial/pallas_call | solution.py:267
  137.3 28.0 %result_scatter.1 = f32[32,8192]{1,0:T(8,128)} custom-call(bf16[4,64,32,128]{3,2,1,0:T(8,128)(2,1)} %cube_partial.1.part), custom_call_target="tpu_custom_call" | custom-call | tf_op jit(solution)/shard_map/result_scatter/pallas_call | solution.py:315
  165.3 2.3 %copy.6 = f32[32,8192]{1,0:T(8,128)} copy(f32[32,8192]{1,0:T(8,128)} %result_scatter.1) | data formatting | bytes 2097152

commit v2 on v1

--- a/solution.py
+++ b/solution.py
@@ -130,102 +130,200 @@
     )(tiles, padded)
 
 
-def first_kernel(block, slots, left_cols, panel_cols, left, tiles, out, dense):
-    step = pl.program_id(0)
-
-    @pl.when(step == 0)
-    def _():
-        dense[...] = jnp.zeros_like(dense)
-        for k in range(slots):
-            dense[left_cols[k]] = left[k]
-
-    for r in range(block):
-        base = (step * block + r) * slots
-        picked = jnp.concatenate([dense[panel_cols[base + k]] for k in range(slots)], axis=1)
-        held = jnp.concatenate([tiles[r, k] for k in range(slots)], axis=1)
+def first_kernel(
+    slots, pairs, left_cols, panel_cols, left, panel, out, rows_out,
+    inverse, place, which, stage, sem,
+):
+    groups, height = out.shape[0], out.shape[2]
+
+    @pl.loop(0, inverse.shape[0])
+    def _(c):
+        inverse[c] = -1
+
+    @pl.loop(0, rows_out.shape[1])
+    def _(c):
+        rows_out[0, c] = 0
+
+    for k in range(slots):
+        inverse[left_cols[k]] = k
+
+    def scan(entry, found):
+        k = inverse[panel_cols[entry]]
+        place[found] = entry
+        which[found] = k
+        return found + (k >= 0).astype(jnp.int32)
+
+    lax.fori_loop(0, panel.shape[0], scan, jnp.int32(0), unroll=8)
+    copies = []
+    for n in range(pairs):
+        copies.append(pltpu.make_async_copy(panel.at[place[n]], stage.at[n], sem.at[n]))
+        copies[-1].start()
+    for n in range(pairs):
+        rows_out[0, n] = lax.div(place[n], jnp.int32(slots))
+        copies[n].wait()
         product = lax.dot_general(
-            picked, held, (((1,), (1,)), ((), ())), preferred_element_type=jnp.float32
-        )
-        out[r] = product.astype(out.dtype)
+            left[which[n]], stage[n], (((1,), (1,)), ((), ())),
+            preferred_element_type=jnp.float32,
+        ).astype(out.dtype)
+        for g in range(groups):
+            out[g, n] = product[g * height:(g + 1) * height]
 
 
 def first(left, left_cols, panel, panel_cols):
     count, slots, size = panel.shape[0], panel.shape[1], panel.shape[2]
-    block = pieces_of(count, 8)
-    return pl.pallas_call(
-        functools.partial(first_kernel, block, slots),
-        out_shape=jax.ShapeDtypeStruct((count, size, size), panel.dtype),
-        grid=(count // block,),
-        in_specs=[
-            pl.BlockSpec(memory_space=pltpu.SMEM),
-            pl.BlockSpec(memory_space=pltpu.SMEM),
-            pl.BlockSpec(left.shape, lambda i: (0, 0, 0)),
-            pl.BlockSpec((block, slots, size, size), lambda i: (i, 0, 0, 0)),
+    pairs = slots * slots
+    groups = lax.axis_size("gz")
+    smem = pl.BlockSpec(memory_space=pltpu.SMEM)
+    vmem = pl.BlockSpec(memory_space=pltpu.VMEM)
+    return pl.pallas_call(
+        functools.partial(first_kernel, slots, pairs),
+        out_shape=(
+            jax.ShapeDtypeStruct((groups, pairs, size // groups, size), panel.dtype),
+            jax.ShapeDtypeStruct((1, LANES), jnp.int32),
+        ),
+        in_specs=[smem, smem, vmem, pl.BlockSpec(memory_space=pl.ANY)],
+        out_specs=(vmem, smem),
+        scratch_shapes=[
+            pltpu.SMEM((count,), jnp.int32),
+            pltpu.SMEM((pairs + 1,), jnp.int32),
+            pltpu.SMEM((pairs + 1,), jnp.int32),
+            pltpu.VMEM((pairs, size, size), panel.dtype),
+            pltpu.SemaphoreType.DMA((pairs,)),
         ],
-        out_specs=pl.BlockSpec((block, size, size), lambda i: (i, 0, 0)),
-        scratch_shapes=[pltpu.VMEM((count, size, size), panel.dtype)],
-        compiler_params=pltpu.CompilerParams(dimension_semantics=("arbitrary",)),
-        name="square_partial",
-    )(left_cols, panel_cols, left, panel)
-
-
-def reduce_kernel(size, pieces, part, own, out, landed, send_a, recv_a, send_b, recv_b):
+        name="square_products",
+    )(left_cols, panel_cols, left, panel.reshape(count * slots, size, size))
+
+
+def exchange_kernel(size, part, rows, landed, rows_landed, own, send, recv, row_send, row_recv):
     me = lax.axis_index("gz")
-    step_rows = part.shape[0] // size
-    rows = step_rows // pieces
     greet(("gz",))
-    scatters, gathers = [], []
+    copies = [
+        pltpu.make_async_copy(part.at[me], landed.at[me], own.at[0]),
+        pltpu.make_async_copy(rows, rows_landed.at[me], own.at[1]),
+    ]
+    for d in range(1, size):
+        peer = lax.rem(me + d, size)
+        copies.append(remote(part.at[peer], landed.at[me], send.at[d - 1], recv.at[d - 1], "gz", peer))
+        copies.append(
+            remote(rows, rows_landed.at[me], row_send.at[d - 1], row_recv.at[d - 1], "gz", peer)
+        )
+    for copy in copies:
+        copy.start()
+    for copy in copies:
+        copy.wait()
+
+
+def exchange(part, rows):
+    size = lax.axis_size("gz")
+    dma = pltpu.SemaphoreType.DMA
+    vmem = pl.BlockSpec(memory_space=pltpu.VMEM)
+    return pl.pallas_call(
+        functools.partial(exchange_kernel, size),
+        out_shape=(
+            jax.ShapeDtypeStruct(part.shape, part.dtype),
+            jax.ShapeDtypeStruct((size,) + rows.shape, rows.dtype),
+        ),
+        in_specs=[vmem, vmem],
+        out_specs=(vmem, vmem),
+        scratch_shapes=[dma((2,))] + [dma((size - 1,))] * 4,
+        compiler_params=pltpu.CompilerParams(collective_id=1, has_side_effects=True),
+        name="square_exchange",
+    )(part, rows)
+
+
+def sum_kernel(rows, landed, out, total):
+    total[...] = jnp.zeros_like(total)
+    for b in range(landed.shape[0]):
+        for n in range(landed.shape[1]):
+            total[rows[b, 0, n]] += landed[b, n].astype(jnp.float32)
+    out[...] = total[...].astype(out.dtype)
+
+
+def sum_products(landed, rows, count):
+    shape = (count,) + landed.shape[2:]
+    vmem = pl.BlockSpec(memory_space=pltpu.VMEM)
+    return pl.pallas_call(
+        sum_kernel,
+        out_shape=jax.ShapeDtypeStruct(shape, landed.dtype),
+        in_specs=[pl.BlockSpec(memory_space=pltpu.SMEM), vmem],
+        out_specs=vmem,
+        scratch_shapes=[pltpu.VMEM(shape, jnp.float32)],
+        name="square_sum",
+    )(rows, landed)
+
+
+def spread_kernel(size, pieces, chunk, out, own, send, recv):
+    me = lax.axis_index("gz")
+    rows = chunk.shape[0] // pieces
+    greet(("gz",))
+    keep = pltpu.make_async_copy(chunk, out.at[me], own)
+    keep.start()
+
+    def hop(side, step, p):
+        way = 1 - 2 * side
+        block = me - way * step
+        span = pl.ds(p * rows, rows)
+        source = chunk.at[span] if step == 0 else out.at[block, span]
+        copy = remote(source, out.at[block, span], send.at[side, step, p], recv.at[side, step, p],
+                      "gz", lax.rem(me + way + size, size))
+        ahead = me + way
+        valid = (block >= 0) & (block < size) & (ahead >= 0) & (ahead < size)
+        return copy, valid
+
+    def landing(side, step, p):
+        way = 1 - 2 * side
+        block = me - way * (step + 1)
+        span = pl.ds(p * rows, rows)
+        copy = remote(out.at[block, span], out.at[block, span], send.at[side, step, p],
+                      recv.at[side, step, p], "gz", lax.rem(me + way + size, size))
+        return copy, (block >= 0) & (block < size)
+
+    def send_hop(side, step, p):
+        copy, valid = hop(side, step, p)
+
+        @pl.when(valid)
+        def _():
+            copy.start()
+
     for p in range(pieces):
-        for d in range(1, size):
-            peer = lax.rem(me + d, size)
-            copy = remote(
-                part.at[pl.ds(peer * step_rows + p * rows, rows)], landed.at[d - 1, p],
-                send_a.at[d - 1, p], recv_a.at[d - 1, p], "gz", peer,
-            )
-            copy.start()
-            scatters.append(copy)
-    for p in range(pieces):
-        for d in range(1, size):
-            scatters[p * (size - 1) + d - 1].wait_recv()
-        start = me * step_rows + p * rows
-        for r in range(rows):
-            total = part[start + r].astype(jnp.float32)
-            for d in range(1, size):
-                total = total + landed[d - 1, p, r].astype(jnp.float32)
-            out[start + r] = total.astype(out.dtype)
-        span = pl.ds(start, rows)
-        for d in range(1, size):
-            copy = remote(
-                out.at[span], out.at[span],
-                send_b.at[d - 1, p], recv_b.at[d - 1, p], "gz", lax.rem(me + d, size),
-            )
-            copy.start()
-            gathers.append(copy)
-    for copy in scatters:
-        copy.wait_send()
-    for copy in gathers:
-        copy.wait()
-
-
-def reduce_square(part):
+        for side in range(2):
+            send_hop(side, 0, p)
+    for step in range(size - 1):
+        for p in range(pieces):
+            for side in range(2):
+                copy, valid = landing(side, step, p)
+
+                @pl.when(valid)
+                def _():
+                    copy.wait_recv()
+
+                if step + 1 < size - 1:
+                    send_hop(side, step + 1, p)
+    for step in range(size - 1):
+        for p in range(pieces):
+            for side in range(2):
+                copy, valid = hop(side, step, p)
+
+                @pl.when(valid)
+                def _():
+                    copy.wait_send()
+    keep.wait()
+
+
+def spread(chunk):
     size = lax.axis_size("gz")
-    step_rows = part.shape[0] // size
-    pieces = pieces_of(step_rows, 4)
+    pieces = pieces_of(chunk.shape[0], 4)
     dma = pltpu.SemaphoreType.DMA
-    landed = (size - 1, pieces, step_rows // pieces) + part.shape[1:]
-
-    def body(part_ref, out, landed_ref, *sems):
-        reduce_kernel(size, pieces, part_ref, None, out, landed_ref, *sems)
-
-    return pl.pallas_call(
-        body,
-        out_shape=jax.ShapeDtypeStruct(part.shape, part.dtype),
-        in_specs=[pl.BlockSpec(memory_space=pltpu.VMEM)],
-        out_specs=pl.BlockSpec(memory_space=pltpu.VMEM),
-        scratch_shapes=[pltpu.VMEM(landed, part.dtype)] + [dma((size - 1, pieces))] * 4,
-        compiler_params=pltpu.CompilerParams(collective_id=1, has_side_effects=True),
-        name="square_reduce",
-    )(part)
+    vmem = pl.BlockSpec(memory_space=pltpu.VMEM)
+    return pl.pallas_call(
+        functools.partial(spread_kernel, size, pieces),
+        out_shape=jax.ShapeDtypeStruct((size,) + chunk.shape, chunk.dtype),
+        in_specs=[vmem],
+        out_specs=vmem,
+        scratch_shapes=[dma, dma((2, size - 1, pieces)), dma((2, size - 1, pieces))],
+        compiler_params=pltpu.CompilerParams(collective_id=3, has_side_effects=True),
+        name="square_spread",
+    )(chunk)
 
 
 def second_kernel(block, slots, groups, panel_cols, square, tiles, out, total):
@@ -233,6 +331,9 @@
     count = total.shape[0]
     height = total.shape[1] // groups
 
+    def rows_of(c):
+        return jnp.concatenate([square[q, c] for q in range(square.shape[0])], axis=0)
+
     @pl.when(step == 0)
     def _():
         total[...] = jnp.zeros_like(total)
@@ -240,9 +341,10 @@
     for r in range(block):
         row = step * block + r
         base = row * slots
+        rounded = rows_of(row)
         for k in range(0, slots, 2):
             held = jnp.concatenate([tiles[r, j] for j in range(k, min(k + 2, slots))], axis=1)
-            product = jnp.dot(square[row], held, preferred_element_type=jnp.float32)
+            product = jnp.dot(rounded, held, preferred_element_type=jnp.float32)
             for j in range(k, min(k + 2, slots)):
                 width = tiles.shape[3]
                 total[panel_cols[base + j]] += product[:, (j - k) * width:(j - k + 1) * width]
@@ -253,7 +355,7 @@
 
         @pl.loop(0, count)
         def _(c):
-            value = (3.0 * same) * square[c].astype(jnp.float32) - 2.0 * total[c]
+            value = (3.0 * same) * rows_of(c).astype(jnp.float32) - 2.0 * total[c]
             value = value.astype(out.dtype)
             for g in range(groups):
                 out[g, c] = value[g * height:(g + 1) * height]
@@ -270,7 +372,7 @@
         grid=(count // block,),
         in_specs=[
             pl.BlockSpec(memory_space=pltpu.SMEM),
-            pl.BlockSpec(square.shape, lambda i: (0, 0, 0)),
+            pl.BlockSpec(square.shape, lambda i: (0, 0, 0, 0)),
             pl.BlockSpec((block, slots, size, size), lambda i: (i, 0, 0, 0)),
         ],
         out_specs=pl.BlockSpec(shape, lambda i: (0, 0, 0, 0)),
@@ -333,8 +435,9 @@
     panel, panel_cols, left, left_cols = gather(tiles, cols)
     panel_cols = panel_cols[:, :, :slots].reshape(-1)
     left_cols = left_cols[0, :slots]
-    part = first(left[0], left_cols, panel, panel_cols)
-    square = reduce_square(part)
+    part, rows = first(left[0], left_cols, panel, panel_cols)
+    landed, rows = exchange(part, rows)
+    square = spread(sum_products(landed, rows, panel.shape[0]))
     return scatter_result(second(square, panel, panel_cols))
 
 

time: 169 us -> 148 us (0.88)
  Pallas kernels: 161 us -> 141 us
    pallas_call x2 -> x4, Pallas kernels: 106 us -> 87.1 us  [the longest x1 45.8 us: spread(): pl.pallas_call(functools.partial(spread_kernel, size, pieces), out_shape=...]
where the time goes in v2:
time: 148 us; the launch traced here: 147 us
  Pallas kernels  141 us (95%)
  local copies, waits for them, and re-layouts  6.29 us (4%)
    pallas_call x1, Pallas kernels, spread(): pl.pallas_call(functools.partial(spread_kernel, size, pieces), out_shape=...  45.8 us
    pallas_call x1, Pallas kernels, scatter_result(): pl.pallas_call(functools.partial(scatter_kernel, size, pieces), out_shape...  26.7 us
    pallas_call x1, Pallas kernels, exchange(): pl.pallas_call(functools.partial(exchange_kernel, size), out_shape=(jax.S...  26.6 us
    pallas_call x1, Pallas kernels, gather(): pl.pallas_call(functools.partial(gather_kernel, n_gx, n_gy, pieces), out_...  15 us
    pallas_call x1, Pallas kernels, second(): pl.pallas_call(functools.partial(second_kernel, block, slots, groups), ou...  12.3 us
    pallas_call x1, Pallas kernels, first(): pl.pallas_call(functools.partial(first_kernel, slots, pairs), out_shape=(...  11.7 us
    unnamed x2, local copies, waits for them, and re-layouts  3.03 us

profile of v2, /device:TPU:0, one launch (start us, length us, event | category | flops | bytes accessed | tf_op | source)
XLA Modules:
  0.0 147.4 jit_solution(8464627278862787701)
XLA Ops:
  0.0 0.8 copy.4
  0.8 0.6 pad.4.cols
  1.4 15.0 %gather_tiles.1 = (bf16[64,6,128,128]{3,2,1,0:T(8,128)(2,1)}, s32[2,32,128]{2,1,0:T(8,128)}, bf16[1,6,128,128]{3,2,1,0:T(8,128)(2,1)}, s32[32,128]{1,0:T(8,128)}) custom-call(bf16[32,6,128,128]{3,2,1,0:T(8,128)(2,1)} %bitcast.8, s32[32,128]{1,0:T(8,128)} %pad.4.cols), custom_call_target="tpu_custom_call" | custom-call | tf_op jit(solution)/shard_map/gather_tiles/pallas_call | solution.py:109
  16.3 1.5 reshape.6.panel_cols
  17.8 1.2 slice_bitcast_fusion.left_cols
  19.0 11.7 %square_products.1 = (bf16[4,36,32,128]{3,2,1,0:T(8,128)(2,1)}, s32[1,128]{1,0:T(1,128)}) custom-call(s32[6]{0:T(128)} %slice_bitcast_fusion.left_cols, s32[384]{0:T(512)} %reshape.6.panel_cols, bf16[6,128,128]{2,1,0:T(8,128)(2,1)} %bitcast.9, bf16[384,128,128]{2,1,0:T(8,128)(2,1)} %bitcast.7), custom_call_target="tpu_custom_call" | custom-call | tf_op jit(solution)/shard_map/square_products/pallas_call | solution.py:178
  30.7 26.6 %square_exchange.1 = (bf16[4,36,32,128]{3,2,1,0:T(8,128)(2,1)}, s32[4,1,128]{2,1,0:T(1,128)}) custom-call(bf16[4,36,32,128]{3,2,1,0:T(8,128)(2,1)} %get-tuple-element.17.part, s32[1,128]{1,0:T(1,128)} %get-tuple-element.18.rows), custom_call_target="tpu_custom_call" | custom-call | tf_op jit(solution)/shard_map/square_exchange/pallas_call | solution.py:220
  57.4 2.9 %square_sum.1.chunk = bf16[64,32,128]{2,1,0:T(8,128)(2,1)} custom-call(s32[4,1,128]{2,1,0:T(1,128)} %get-tuple-element.19.rows, bf16[4,36,32,128]{3,2,1,0:T(8,128)(2,1)} %get-tuple-element.20.landed), custom_call_target="tpu_custom_call" | custom-call | tf_op jit(solution)/shard_map/square_sum/pallas_call | solution.py:245
  60.3 45.8 %square_spread.1.square = bf16[4,64,32,128]{3,2,1,0:T(8,128)(2,1)} custom-call(bf16[64,32,128]{2,1,0:T(8,128)(2,1)} %square_sum.1.chunk), custom_call_target="tpu_custom_call" | custom-call | tf_op jit(solution)/shard_map/square_spread/pallas_call | solution.py:318
  106.1 12.3 %cube_partial.1.part = bf16[4,64,32,128]{3,2,1,0:T(8,128)(2,1)} custom-call(s32[384]{0:T(512)} %reshape.6.panel_cols, bf16[4,64,32,128]{3,2,1,0:T(8,128)(2,1)} %square_spread.1.square, bf16[64,6,128,128]{3,2,1,0:T(8,128)(2,1)} %get-tuple-element.16.tiles), custom_call_target="tpu_custom_call" | custom-call | tf_op jit(solution)/shard_map/cube_partial/pallas_call | solution.py:369
  118.4 26.7 %result_scatter.1 = f32[32,8192]{1,0:T(8,128)} custom-call(bf16[4,64,32,128]{3,2,1,0:T(8,128)(2,1)} %cube_partial.1.part), custom_call_target="tpu_custom_call" | custom-call | tf_op jit(solution)/shard_map/result_scatter/pallas_call | solution.py:417
  145.1 2.3 %copy.6 = f32[32,8192]{1,0:T(8,128)} copy(f32[32,8192]{1,0:T(8,128)} %result_scatter.1) | data formatting | bytes 2097152

commit v3 on v2

--- a/solution.py
+++ b/solution.py
@@ -136,37 +136,43 @@
 ):
     groups, height = out.shape[0], out.shape[2]
 
-    @pl.loop(0, inverse.shape[0])
-    def _(c):
+    for c in range(inverse.shape[0]):
         inverse[c] = -1
-
-    @pl.loop(0, rows_out.shape[1])
-    def _(c):
+    for c in range(pairs, rows_out.shape[1]):
         rows_out[0, c] = 0
-
     for k in range(slots):
         inverse[left_cols[k]] = k
-
-    def scan(entry, found):
-        k = inverse[panel_cols[entry]]
-        place[found] = entry
-        which[found] = k
-        return found + (k >= 0).astype(jnp.int32)
-
-    lax.fori_loop(0, panel.shape[0], scan, jnp.int32(0), unroll=8)
+    entries = panel.shape[0]
+    group = pieces_of(entries, 32)
+
+    def scan(step, found):
+        base = step * group
+        matches = [inverse[panel_cols[base + j]] for j in range(group)]
+        for j, k in enumerate(matches):
+            place[found] = base + j
+            which[found] = k
+            found = found + (k >= 0).astype(jnp.int32)
+        return found
+
+    lax.fori_loop(0, entries // group, scan, jnp.int32(0))
+    bunch = pairs // pieces_of(pairs, 4)
     copies = []
     for n in range(pairs):
         copies.append(pltpu.make_async_copy(panel.at[place[n]], stage.at[n], sem.at[n]))
         copies[-1].start()
     for n in range(pairs):
         rows_out[0, n] = lax.div(place[n], jnp.int32(slots))
-        copies[n].wait()
-        product = lax.dot_general(
-            left[which[n]], stage[n], (((1,), (1,)), ((), ())),
-            preferred_element_type=jnp.float32,
-        ).astype(out.dtype)
-        for g in range(groups):
-            out[g, n] = product[g * height:(g + 1) * height]
+    for first_pair in range(0, pairs, bunch):
+        span = range(first_pair, first_pair + bunch)
+        for n in span:
+            copies[n].wait()
+        for n in span:
+            product = lax.dot_general(
+                left[which[n]], stage[n], (((1,), (1,)), ((), ())),
+                preferred_element_type=jnp.float32,
+            ).astype(out.dtype)
+            for g in range(groups):
+                out[g, n] = product[g * height:(g + 1) * height]
 
 
 def first(left, left_cols, panel, panel_cols):

time: 148 us -> 143 us (0.966)
  Pallas kernels: 141 us -> 136 us
    pallas_call x1, Pallas kernels: 11.7 us -> 6.33 us  [first(): pl.pallas_call(functools.partial(first_kernel, slots, pairs), out_shape=(...]
where the time goes in v3:
time: 143 us; the launch traced here: 142 us
  Pallas kernels  136 us (95%)
  local copies, waits for them, and re-layouts  6.29 us (4%)
    pallas_call x1, Pallas kernels, spread(): pl.pallas_call(functools.partial(spread_kernel, size, pieces), out_shape=...  45.8 us
    pallas_call x1, Pallas kernels, scatter_result(): pl.pallas_call(functools.partial(scatter_kernel, size, pieces), out_shape...  26.7 us
    pallas_call x1, Pallas kernels, exchange(): pl.pallas_call(functools.partial(exchange_kernel, size), out_shape=(jax.S...  26.7 us
    pallas_call x1, Pallas kernels, gather(): pl.pallas_call(functools.partial(gather_kernel, n_gx, n_gy, pieces), out_...  15 us
    pallas_call x1, Pallas kernels, second(): pl.pallas_call(functools.partial(second_kernel, block, slots, groups), ou...  12.3 us
    pallas_call x1, Pallas kernels, first(): pl.pallas_call(functools.partial(first_kernel, slots, pairs), out_shape=(...  6.33 us
    unnamed x2, local copies, waits for them, and re-layouts  3.03 us
    pallas_call x1, Pallas kernels, sum_products(): pl.pallas_call(sum_kernel, out_shape=jax.ShapeDtypeStruct(shape, landed.d...  2.91 us

profile of v3, /device:TPU:0, one launch (start us, length us, event | category | flops | bytes accessed | tf_op | source)
XLA Modules:
  0.0 142.0 jit_solution(12587528451976360446)
XLA Ops:
  0.0 0.8 copy.4
  0.8 0.6 pad.4.cols
  1.4 15.0 %gather_tiles.1 = (bf16[64,6,128,128]{3,2,1,0:T(8,128)(2,1)}, s32[2,32,128]{2,1,0:T(8,128)}, bf16[1,6,128,128]{3,2,1,0:T(8,128)(2,1)}, s32[32,128]{1,0:T(8,128)}) custom-call(bf16[32,6,128,128]{3,2,1,0:T(8,128)(2,1)} %bitcast.8, s32[32,128]{1,0:T(8,128)} %pad.4.cols), custom_call_target="tpu_custom_call" | custom-call | tf_op jit(solution)/shard_map/gather_tiles/pallas_call | solution.py:109
  16.3 1.5 %reshape.6.panel_cols = s32[384]{0:T(512)} reshape(s32[2,32,6]{2,1,0:T(8,128)} %bitcast.11) | data formatting | bytes 3072 | tf_op jit(solution)/shard_map/reshape | solution.py:442
  17.8 1.2 slice_bitcast_fusion.left_cols
  19.0 6.3 %square_products.1 = (bf16[4,36,32,128]{3,2,1,0:T(8,128)(2,1)}, s32[1,128]{1,0:T(1,128)}) custom-call(s32[6]{0:T(128)} %slice_bitcast_fusion.left_cols, s32[384]{0:T(512)} %reshape.6.panel_cols, bf16[6,128,128]{2,1,0:T(8,128)(2,1)} %bitcast.9, bf16[384,128,128]{2,1,0:T(8,128)(2,1)} %bitcast.7), custom_call_target="tpu_custom_call" | custom-call | tf_op jit(solution)/shard_map/square_products/pallas_call | solution.py:184
  25.3 26.7 %square_exchange.1 = (bf16[4,36,32,128]{3,2,1,0:T(8,128)(2,1)}, s32[4,1,128]{2,1,0:T(1,128)}) custom-call(bf16[4,36,32,128]{3,2,1,0:T(8,128)(2,1)} %get-tuple-element.17.part, s32[1,128]{1,0:T(1,128)} %get-tuple-element.18.rows), custom_call_target="tpu_custom_call" | custom-call | tf_op jit(solution)/shard_map/square_exchange/pallas_call | solution.py:226
  52.0 2.9 %square_sum.1.chunk = bf16[64,32,128]{2,1,0:T(8,128)(2,1)} custom-call(s32[4,1,128]{2,1,0:T(1,128)} %get-tuple-element.19.rows, bf16[4,36,32,128]{3,2,1,0:T(8,128)(2,1)} %get-tuple-element.20.landed), custom_call_target="tpu_custom_call" | custom-call | tf_op jit(solution)/shard_map/square_sum/pallas_call | solution.py:251
  54.9 45.8 %square_spread.1.square = bf16[4,64,32,128]{3,2,1,0:T(8,128)(2,1)} custom-call(bf16[64,32,128]{2,1,0:T(8,128)(2,1)} %square_sum.1.chunk), custom_call_target="tpu_custom_call" | custom-call | tf_op jit(solution)/shard_map/square_spread/pallas_call | solution.py:324
  100.8 12.3 %cube_partial.1.part = bf16[4,64,32,128]{3,2,1,0:T(8,128)(2,1)} custom-call(s32[384]{0:T(512)} %reshape.6.panel_cols, bf16[4,64,32,128]{3,2,1,0:T(8,128)(2,1)} %square_spread.1.square, bf16[64,6,128,128]{3,2,1,0:T(8,128)(2,1)} %get-tuple-element.16.tiles), custom_call_target="tpu_custom_call" | custom-call | tf_op jit(solution)/shard_map/cube_partial/pallas_call | solution.py:375
  113.1 26.7 %result_scatter.1 = f32[32,8192]{1,0:T(8,128)} custom-call(bf16[4,64,32,128]{3,2,1,0:T(8,128)(2,1)} %cube_partial.1.part), custom_call_target="tpu_custom_call" | custom-call | tf_op jit(solution)/shard_map/result_scatter/pallas_call | solution.py:423
  139.8 2.3 %copy.6 = f32[32,8192]{1,0:T(8,128)} copy(f32[32,8192]{1,0:T(8,128)} %result_scatter.1) | data formatting | bytes 2097152

commit v4 on v3

--- a/solution.py
+++ b/solution.py
@@ -141,7 +141,7 @@
     for c in range(pairs, rows_out.shape[1]):
         rows_out[0, c] = 0
     for k in range(slots):
-        inverse[left_cols[k]] = k
+        inverse[left_cols[0, k]] = k
     entries = panel.shape[0]
     group = pieces_of(entries, 32)
 
@@ -318,7 +318,7 @@
 
 def spread(chunk):
     size = lax.axis_size("gz")
-    pieces = pieces_of(chunk.shape[0], 4)
+    pieces = pieces_of(chunk.shape[0], 8)
     dma = pltpu.SemaphoreType.DMA
     vmem = pl.BlockSpec(memory_space=pltpu.VMEM)
     return pl.pallas_call(
@@ -418,7 +418,7 @@
 def scatter_result(part):
     size = lax.axis_size("gy")
     count, height, width = part.shape[1:]
-    pieces = pieces_of(count, 4)
+    pieces = pieces_of(count, 8)
     dma = pltpu.SemaphoreType.DMA
     return pl.pallas_call(
         functools.partial(scatter_kernel, size, pieces),
@@ -440,7 +440,6 @@
     slots = cols.shape[1]
     panel, panel_cols, left, left_cols = gather(tiles, cols)
     panel_cols = panel_cols[:, :, :slots].reshape(-1)
-    left_cols = left_cols[0, :slots]
     part, rows = first(left[0], left_cols, panel, panel_cols)
     landed, rows = exchange(part, rows)
     square = spread(sum_products(landed, rows, panel.shape[0]))

time: 143 us -> 142 us (level)
  no operation moved by 1% of the time
where the time goes in v4:
time: 142 us
  Pallas kernels  136 us (96%)
  local copies, waits for them, and re-layouts  5.1 us (4%)
    pallas_call x1, Pallas kernels, spread(): pl.pallas_call(functools.partial(spread_kernel, size, pieces), out_shape=...  46.3 us
    pallas_call x1, Pallas kernels, scatter_result(): pl.pallas_call(functools.partial(scatter_kernel, size, pieces), out_shape...  26.9 us
    pallas_call x1, Pallas kernels, exchange(): pl.pallas_call(functools.partial(exchange_kernel, size), out_shape=(jax.S...  26.6 us
    pallas_call x1, Pallas kernels, gather(): pl.pallas_call(functools.partial(gather_kernel, n_gx, n_gy, pieces), out_...  15 us
    pallas_call x1, Pallas kernels, second(): pl.pallas_call(functools.partial(second_kernel, block, slots, groups), ou...  12.3 us
    pallas_call x1, Pallas kernels, first(): pl.pallas_call(functools.partial(first_kernel, slots, pairs), out_shape=(...  6.35 us
    unnamed x2, local copies, waits for them, and re-layouts  3.03 us
    pallas_call x1, Pallas kernels, sum_products(): pl.pallas_call(sum_kernel, out_shape=jax.ShapeDtypeStruct(shape, landed.d...  2.91 us

profile of v4, /device:TPU:0, one launch (start us, length us, event | category | flops | bytes accessed | tf_op | source)
XLA Modules:
  0.0 141.5 jit_solution(13044209011951206779)
XLA Ops:
  0.0 0.8 copy.4
  0.8 0.6 pad.4.cols
  1.4 15.0 %gather_tiles.1 = (bf16[64,6,128,128]{3,2,1,0:T(8,128)(2,1)}, s32[2,32,128]{2,1,0:T(8,128)}, bf16[1,6,128,128]{3,2,1,0:T(8,128)(2,1)}, s32[32,128]{1,0:T(8,128)}) custom-call(bf16[32,6,128,128]{3,2,1,0:T(8,128)(2,1)} %bitcast.6, s32[32,128]{1,0:T(8,128)} %pad.4.cols), custom_call_target="tpu_custom_call" | custom-call | tf_op jit(solution)/shard_map/gather_tiles/pallas_call | solution.py:109
  16.3 1.5 %reshape.6.panel_cols = s32[384]{0:T(512)} reshape(s32[2,32,6]{2,1,0:T(8,128)} %bitcast.9) | data formatting | bytes 3072 | tf_op jit(solution)/shard_map/reshape | solution.py:442
  17.8 6.4 %square_products.1 = (bf16[4,36,32,128]{3,2,1,0:T(8,128)(2,1)}, s32[1,128]{1,0:T(1,128)}) custom-call(s32[32,128]{1,0:T(8,128)} %get-tuple-element.14.left_cols, s32[384]{0:T(512)} %reshape.6.panel_cols, bf16[6,128,128]{2,1,0:T(8,128)(2,1)} %bitcast.7, bf16[384,128,128]{2,1,0:T(8,128)(2,1)} %bitcast.5), custom_call_target="tpu_custom_call" | custom-call | tf_op jit(solution)/shard_map/square_products/pallas_call | solution.py:184
  24.2 26.6 %square_exchange.1 = (bf16[4,36,32,128]{3,2,1,0:T(8,128)(2,1)}, s32[4,1,128]{2,1,0:T(1,128)}) custom-call(bf16[4,36,32,128]{3,2,1,0:T(8,128)(2,1)} %get-tuple-element.17.part, s32[1,128]{1,0:T(1,128)} %get-tuple-element.18.rows), custom_call_target="tpu_custom_call" | custom-call | tf_op jit(solution)/shard_map/square_exchange/pallas_call | solution.py:226
  50.8 2.9 %square_sum.1.chunk = bf16[64,32,128]{2,1,0:T(8,128)(2,1)} custom-call(s32[4,1,128]{2,1,0:T(1,128)} %get-tuple-element.19.rows, bf16[4,36,32,128]{3,2,1,0:T(8,128)(2,1)} %get-tuple-element.20.landed), custom_call_target="tpu_custom_call" | custom-call | tf_op jit(solution)/shard_map/square_sum/pallas_call | solution.py:251
  53.7 46.3 %square_spread.1.square = bf16[4,64,32,128]{3,2,1,0:T(8,128)(2,1)} custom-call(bf16[64,32,128]{2,1,0:T(8,128)(2,1)} %square_sum.1.chunk), custom_call_target="tpu_custom_call" | custom-call | tf_op jit(solution)/shard_map/square_spread/pallas_call | solution.py:324
  100.0 12.3 %cube_partial.1.part = bf16[4,64,32,128]{3,2,1,0:T(8,128)(2,1)} custom-call(s32[384]{0:T(512)} %reshape.6.panel_cols, bf16[4,64,32,128]{3,2,1,0:T(8,128)(2,1)} %square_spread.1.square, bf16[64,6,128,128]{3,2,1,0:T(8,128)(2,1)} %get-tuple-element.16.tiles), custom_call_target="tpu_custom_call" | custom-call | tf_op jit(solution)/shard_map/cube_partial/pallas_call | solution.py:375
  112.4 26.9 %result_scatter.1 = f32[32,8192]{1,0:T(8,128)} custom-call(bf16[4,64,32,128]{3,2,1,0:T(8,128)(2,1)} %cube_partial.1.part), custom_call_target="tpu_custom_call" | custom-call | tf_op jit(solution)/shard_map/result_scatter/pallas_call | solution.py:423
  139.3 2.3 %copy.6 = f32[32,8192]{1,0:T(8,128)} copy(f32[32,8192]{1,0:T(8,128)} %result_scatter.1) | data formatting | bytes 2097152
